TPU v7x, 32 devices: a whole 2x2x4 slice. The times are simulated.
32 devices in a mesh: groups: 2 (over x), row: 8 (over z, y), head: 2 (over core).
Axes of the slice: x: 2, y: 2, z: 4, core: 2. Of those that a mesh axis runs over, the one named last changes fastest.
Arguments:
- hidden: bfloat16 [48, 4096], P('groups'), parts along dimension 0, may hold values from -6 to 6
- norm_gain: float32 [4096], replicated, may hold values from 0.1 to 1.9
- w_query: bfloat16 [8, 256, 4096], P('head', 'row'), may hold values from -0.09375 to 0.09375
- w_key: bfloat16 [8, 256, 4096], P('head', 'row'), may hold values from -0.09375 to 0.09375
- w_value: bfloat16 [8, 512, 4096], P('head', 'row'), may hold values from -0.09375 to 0.09375
- w_outgate: bfloat16 [8, 512, 4096], P('head', 'row'), may hold values from -0.09375 to 0.09375
- w_out: bfloat16 [8, 512, 4096], P('head', 'row'), may hold values from -0.125 to 0.125
- w_gates: bfloat16 [2, 8, 4096], P(None, 'head'), may hold values from -0.09375 to 0.09375
- gate_bias: float32 [2, 8], P(None, 'head'), may hold values from -2 to 4
- headnorm_gain: float32 [8, 512], P('head', 'row'), may hold values from 0.1 to 1.9
- final_gain: float32 [4096], replicated, may hold values from 0.1 to 1.9
- w_vocab: bfloat16 [25152, 4096], P(('row', 'head')), may hold values from -39.0625 to 39.0625
- memory: float32 [48, 8, 256, 512], P('groups', 'head', 'row'), parts along dimension 0, may hold values from -6 to 6
- normalizer: float32 [48, 8, 256], P('groups', 'head', 'row'), parts along dimension 0, may hold values from -6 to 6
- stabilizer: float32 [48, 8], P('groups', 'head'), parts along dimension 0, may hold values from -2 to 2
- targets: int32 [48], P('groups'), parts along dimension 0, may hold values from 0 to 25151
Outputs:
- memory_out: float32 [48, 8, 256, 512], P('groups', 'head', 'row'), parts along dimension 0
- normalizer_out: float32 [48, 8, 256], P('groups', 'head', 'row'), parts along dimension 0
- stabilizer_out: float32 [48, 8], P('groups', 'head'), parts along dimension 0
- hidden_out: bfloat16 [48, 4096], P('groups', ('row', 'head')), parts along dimension 0
- log_prob: float32 [48], P('groups'), parts along dimension 0
There are 2 independent parts, one for each index of `groups`. A program takes and returns all parts, laid end to end along the dimension named above; an argument that names none is the same for every part. Nothing has to cross between parts.
All inputs are finite; a program needn't handle non-finite values.
Results may differ from a plain program's by a relative error of at most 0.0035.
The roundings to bfloat16 on the way count: a program that leaves them out, or rounds other values in their place, can miss the bound.
Values may be sent and summed in bfloat16 or wider, within the bound.
A program may use at most 64 MiB of HBM per device.

v0:
```python
import math
import jax
import jax.numpy as jnp
from jax import lax
from jax.sharding import PartitionSpec as P

QK_DIM = 256
epsilon = 1e-06


def joined_2(value, axis, join):
    pieces = jax.tree.map(lambda part: lax.all_gather(part, axis), value)
    head = jax.tree.map(lambda part: part[0], pieces)
    tail = jax.tree.map(lambda part: part[1:], pieces)
    total, _ = lax.scan(lambda total, share: (join(total, share), None), head, tail)
    return total


def rms_round(stream, gain):
    scale = lax.rsqrt(jnp.mean(stream * stream, axis=-1, keepdims=True) + epsilon)
    return (stream * scale * gain).astype(jnp.bfloat16)


def per_device(
    hidden,
    norm_gain,
    w_query,
    w_key,
    w_value,
    w_outgate,
    w_out,
    w_gates,
    gate_bias,
    headnorm_gain,
    final_gain,
    w_vocab,
    memory,
    normalizer,
    stabilizer,
    targets,
):
    value_rows = w_value.shape[1]
    stream = hidden.astype(jnp.float32)
    normed_in = rms_round(stream, norm_gain)

    def project(weights):
        return jnp.einsum("sd,hjd->shj", normed_in, weights, preferred_element_type=jnp.float32)

    queries = project(w_query) / math.sqrt(QK_DIM)
    key_part = project(w_key)
    value_part = project(w_value).astype(jnp.bfloat16)
    outgate_pre = project(w_outgate)
    gate_pre = (
        jnp.einsum("sd,ghd->gsh", normed_in, w_gates, preferred_element_type=jnp.float32)
        + gate_bias[:, None, :]
    )
    log_forget = jax.nn.log_sigmoid(gate_pre[1])
    stabilizer_out = jnp.maximum(log_forget + stabilizer, gate_pre[0])
    decay_rate = jnp.exp(log_forget + stabilizer - stabilizer_out)
    inflow = jnp.exp(gate_pre[0] - stabilizer_out)
    scaled_key = inflow[:, :, None] * key_part
    memory_out = (
        decay_rate[:, :, None, None] * memory
        + scaled_key[:, :, :, None]
        * lax.all_gather(value_part, "row", axis=2, tiled=True).astype(jnp.float32)[:, :, None, :]
    )
    normalizer_out = decay_rate[:, :, None] * normalizer + scaled_key
    partial_readout = jnp.einsum(
        "shj,shje->she", queries, memory_out, precision=lax.Precision.HIGHEST
    )
    readout = lax.psum(partial_readout, "row")
    average = jnp.mean(readout, axis=-1)
    centered_full = readout - average[:, :, None]
    variance = jnp.mean(centered_full * centered_full, axis=-1)
    centered = lax.dynamic_slice_in_dim(
        centered_full, lax.axis_index("row") * value_rows, value_rows, 2
    )
    normed = centered * lax.rsqrt(variance + epsilon)[:, :, None] * headnorm_gain
    gated_out = (jax.nn.sigmoid(outgate_pre) * normed).astype(jnp.bfloat16)
    partial_terms = jnp.einsum("shj,hjd->sd", gated_out, w_out, preferred_element_type=jnp.float32)
    position = lax.axis_index("row") * lax.axis_size("head") + lax.axis_index("head")
    share_width = hidden.shape[1] // (lax.axis_size("row") * lax.axis_size("head"))
    vocab_here = w_vocab.shape[0]
    projection = lax.psum(partial_terms, ("row", "head"))
    new_full = (stream + projection).astype(jnp.bfloat16)
    final_feat = rms_round(new_full.astype(jnp.float32), final_gain)
    logits = jnp.einsum("sd,vd->sv", final_feat, w_vocab, preferred_element_type=jnp.float32)
    hidden_out = lax.dynamic_slice_in_dim(new_full, position * share_width, share_width, 1)
    local_ids = targets - position * vocab_here
    is_target = jnp.arange(vocab_here, dtype=jnp.int32)[None, :] == local_ids[:, None]
    target_term = jnp.sum(jnp.where(is_target, logits, 0.0), axis=-1)
    local_max = jnp.max(logits, axis=-1)
    local_sum = jnp.sum(jnp.exp(logits - local_max[:, None]), axis=-1)

    def combine(earlier, later):
        highest = jnp.maximum(earlier[0], later[0])
        joined = earlier[1] * jnp.exp(earlier[0] - highest) + later[1] * jnp.exp(later[0] - highest)
        return (highest, joined, earlier[2] + later[2])

    highest, exp_total, picked = joined_2(
        (local_max, local_sum, target_term), ("row", "head"), combine
    )
    log_prob = picked - (highest + jnp.log(exp_total))
    return (memory_out, normalizer_out, stabilizer_out, hidden_out, log_prob)


def solution(mesh):
    in_specs = (
        P("groups", None),
        P(),
        P("head", "row", None),
        P("head", "row", None),
        P("head", "row", None),
        P("head", "row", None),
        P("head", "row", None),
        P(None, "head", None),
        P(None, "head"),
        P("head", "row"),
        P(),
        P(("row", "head"), None),
        P("groups", "head", "row", None),
        P("groups", "head", "row"),
        P("groups", "head"),
        P("groups"),
    )
    out_specs = (
        P("groups", "head", "row", None),
        P("groups", "head", "row"),
        P("groups", "head"),
        P("groups", ("row", "head")),
        P("groups"),
    )
    return jax.shard_map(
        per_device, mesh=mesh, in_specs=in_specs, out_specs=out_specs, check_vma=False
    )
```

profile of v0, /device:TPU:0, one launch (start us, length us, event | category | flops | bytes accessed | tf_op | source)
XLA Modules:
  0.0 280.0 jit_solution(1592682969917463788)
XLA Ops:
  7.2 0.0 copy-start
  7.2 0.0 all-reduce.7.cloned.1.call-start
  7.2 1.2 fusion.17
  8.5 2.7 convolution_convert_fusion
  11.1 0.1 copy.34
  11.3 33.0 %all_gather.21 = bf16[24,4,512]{0,1,2:T(4,128)(2,1)S(1)} all-gather(bf16[24,4,64]{0,1,2:T(4,128)(2,1)S(1)} %copy.34), channel_id=1, replica_groups=mesh['groups'=2,'row'=8,'head'=2] {'row'}, dimensions={2}, use_global_device_ids=true | all-gather | bytes 110592 | tf_op jit(solution)/shard_map/all_gather | solution.py:65
  44.3 0.3 copy.35
  44.6 0.1 copy.36
  44.7 1.2 fusion.13
  45.9 0.7 subtract_exponential_fusion.1
  46.6 0.0 copy-start.5
  46.6 0.1 copy.32
  46.7 2.2 fusion.28
  48.9 2.2 fusion.7
  51.1 3.4 %multiply_add_fusion = f32[24,4,32,512]{3,2,1,0:T(8,128)S(1)} fusion(f32[24,4,32,512]{3,2,1,0:T(8,128)} %param.30, f32[24,4,512]{2,1,0:T(4,128)S(1)} %copy.36, f32[24,4,32]{2,1,0:T(4,128)S(1)} %copy.33, f32[24,4]{1,0:T(8,128)S(1)} %copy.32), kind=kLoop, calls=%fused_computation.10 | loop fusion | flops 4718592 | bytes 12792192 | tf_op jit(solution)/shard_map/add | solution.py:63
  54.5 0.0 copy-start.1
  54.5 2.7 copy-done.1
  57.2 0.0 copy-start.7
  57.2 0.0 copy-start.4
  57.2 3.1 %fusion.26 = f32[24,4,1,512]{3,2,1,0:T(1,128)S(1)} fusion(f32[24,4,32,512]{3,2,1,0:T(8,128)S(1)} %multiply_add_fusion, f32[24,4,32,1]{2,0,1,3:T(8,128)S(1)} %fusion.7), kind=kOutput, calls=%fused_computation.46 | convolution fusion | flops 18874368 | bytes 6500352 | tf_op jit(solution)/shard_map/shj,shje->she/dot_general | solution.py:68
  60.4 0.7 copy.47
  61.1 0.0 all-reduce.7.cloned.1.call-update
  61.1 0.0 all-reduce.9.cloned.1.call-start
  61.2 0.6 copy.38
  61.8 0.6 dynamic-slice
  63.1 70.0 %all-reduce.7.cloned.1.call-done = f32[24,4,512]{2,0,1:T(8,128)} async-done(((f32[24,4,512]{2,0,1:T(8,128)}), f32[24,4,512]{2,0,1:T(8,128)}) %all-reduce.7.cloned.1.call-update) | async-done | bytes 196624 | tf_op jit(solution)/shard_map/psum | solution.py:71
  133.1 1.0 reduce_sum.55
  134.1 1.1 multiply_reduce_fusion
  135.3 3.8 %convolution_bitcast_fusion = f32[24,4096]{1,0:T(8,128)} fusion(bf16[4,64,4096]{2,1,0:T(8,128)(2,1)S(1)} %copy-done, bf16[4,64,4096]{2,1,0:T(8,128)(2,1)} %param.23, f32[24,4,512]{2,0,1:T(8,128)S(1)} %get-tuple-element.86, s32[]{:T(128)S(6)} %select_n.16, f32[4,64]{1,0:T(4,128)S(1)} %copy-done.6, f32[24,4]{0,1:T(4,128)S(1)} %add_rsqrt_fusion, ...), kind=kOutput, calls=%fused_computation.11 | convolution fusion | flops 101099520 | bytes 4854276 | tf_op jit(solution)/shard_map/shj,hjd->sd/dot_general | solution.py:80
  139.0 0.0 all-reduce.9.cloned.1.call-update
  139.1 90.6 %all-reduce.9.cloned.1.call-done = f32[24,4096]{1,0:T(8,128)} async-done(((f32[24,4096]{1,0:T(8,128)}), f32[24,4096]{1,0:T(8,128)}) %all-reduce.9.cloned.1.call-update) | async-done | bytes 393232 | tf_op jit(solution)/shard_map/psum | solution.py:84
  229.6 1.2 fusion.14
  230.8 0.0 copy-done.4
  230.8 8.3 %fusion.50 = (f32[24]{0:T(128)S(1)}, f32[24,1572]{1,0:T(8,128)S(1)}) fusion(bf16[1572,4096]{1,0:T(8,128)(2,1)} %param.29, bf16[24,4096]{1,0:T(8,128)(2,1)S(1)} %get-tuple-element.84, f32[4096]{0:T(1024)S(1)} %copy-done.4, f32[24]{0:T(128)S(1)} %add_rsqrt_fusion.1), kind=kOutput, calls=%fused_computation.74 | convolution fusion | flops 309498688 | bytes 13241920 | tf_op jit(solution)/shard_map/sd,vd->sv/dot_general | solution.py:87
  239.1 0.2 dynamic-update-slice
  239.3 0.2 select_reduce_fusion
  239.6 0.2 dynamic-update-slice.1
  239.8 0.2 dynamic-update-slice.2
  240.0 30.9 %all-reduce.3 = (f32[384]{0:T(512)S(1)}, f32[384]{0:T(512)S(1)}, f32[384]{0:T(512)S(1)}) all-reduce(f32[384]{0:T(512)S(1)} %dynamic-update-slice, f32[384]{0:T(512)S(1)} %dynamic-update-slice.1, f32[384]{0:T(512)S(1)} %dynamic-update-slice.2), channel_id=2, replica_groups=mesh['groups'=2,'row'=8,'head'=2] {'row','head'}, use_global_device_ids=true, to_apply=%add | all-reduce | flops 1152 | bytes 9216
  271.0 0.1 slice.36
  271.0 0.1 slice.37
  271.1 0.1 slice.38
  271.2 0.6 constant_dynamic-slice_fusion.3
  271.8 0.1 reshape.55
  271.9 0.1 reshape.56
  271.9 0.1 reshape.57
  272.0 0.6 while.14
  272.7 0.5 add_subtract_fusion
  (39 shorter events, 0.5 us)
Async XLA Ops:
  7.2 128.1 %copy-start = (bf16[4,64,4096]{2,1,0:T(8,128)(2,1)S(1)}, bf16[4,64,4096]{2,1,0:T(8,128)(2,1)}, u32[]{:S(2)}) copy-start(bf16[4,64,4096]{2,1,0:T(8,128)(2,1)} %param.24) | copy-start | bytes 6291460
  7.2 125.9 %all-reduce.7.cloned.1.call-start = ((), (), s32[]{:S(2)}) async-start(), calls=%async_computation | async-start | bytes 393216 | tf_op jit(solution)/shard_map/psum | solution.py:71
  46.6 7.9 %copy-start.5 = (f32[24,4]{0,1:T(4,128)}, f32[24,4]{0,1:T(4,128)S(1)}, u32[]{:S(2)}) copy-start(f32[24,4]{0,1:T(4,128)S(1)} %get-tuple-element.88) | copy-start | bytes 1156
  54.5 2.7 copy-start.1
  57.2 4.6 %copy-start.8 = (u32[32]{0:T(128)S(1)}, u32[32]{0:T(128)}, u32[]{:S(2)}) copy-start(u32[32]{0:T(128)} %constant.57) | copy-start | bytes 388
  57.2 78.0 %copy-start.2 = (bf16[24,4096]{1,0:T(8,128)(2,1)S(1)}, bf16[24,4096]{1,0:T(8,128)(2,1)}, u32[]{:S(2)}) copy-start(bf16[24,4096]{1,0:T(8,128)(2,1)} %param.18) | copy-start | bytes 589828
  57.2 78.0 %copy-start.3 = (f32[4096]{0:T(1024)S(1)}, f32[4096]{0:T(1024)}, u32[]{:S(2)}) copy-start(f32[4096]{0:T(1024)} %param.19) | copy-start | bytes 49156
  57.2 78.1 %copy-start.6 = (f32[4,64]{1,0:T(4,128)S(1)}, f32[4,64]{1,0:T(4,128)}, u32[]{:S(2)}) copy-start(f32[4,64]{1,0:T(4,128)} %param.27) | copy-start | bytes 3076
  57.2 81.8 %copy-start.7 = (s32[24]{0:T(128)S(1)}, s32[24]{0:T(128)}, u32[]{:S(2)}) copy-start(s32[24]{0:T(128)} %param.33) | copy-start | bytes 292
  57.2 173.6 %copy-start.4 = (f32[4096]{0:T(1024)S(1)}, f32[4096]{0:T(1024)}, u32[]{:S(2)}) copy-start(f32[4096]{0:T(1024)} %param.28) | copy-start | bytes 49156
  61.1 168.5 %all-reduce.9.cloned.1.call-start = ((), (), s32[]{:S(2)}) async-start(), calls=%async_computation.1 | async-start | bytes 786432 | tf_op jit(solution)/shard_map/psum | solution.py:84
Sparse Core Ops, SparseCore 0:
  61.2 71.7 all-reduce.6
  139.2 90.4 all-reduce.8
where the time goes:
time: 281 us; the launch traced here: 280 us
  waiting for transfers between devices  161 us (57%)
  blocking collectives  64 us (23%)
  matrix products  23.4 us (8%)
  between operations  15 us (5%)
  other arithmetic  9.78 us (3%)
  local copies, waits for them, and re-layouts  7.02 us (2%)
    psum x1, waiting for transfers between devices, per_device(): projection = lax.psum(partial_terms, ('row', 'head'))  90.6 us
    psum x1, waiting for transfers between devices, per_device(): readout = lax.psum(partial_readout, 'row')  70 us
    all_gather x1, blocking collectives, per_device(): lax.all_gather(value_part, 'row', axis=2, tiled=True).astype(jnp.float32)  33 us
    unnamed x1, blocking collectives  30.9 us
    dot_general x1, matrix products, per_device(): jnp.einsum('sd,vd->sv', final_feat, w_vocab, preferred_element_type=jnp.f...  8.26 us
    dot_general x3, matrix products, project(): jnp.einsum('sd,hjd->shj', normed_in, weights, preferred_element_type=jnp....  7.03 us
  transfers between devices with their start and end apart: 2, of which 2 were waited for; matrix products, arithmetic and copies ran while one was open for 0% of the time, Pallas kernels for 0%

commit v1 on v0

--- a/solution.py
+++ b/solution.py
@@ -81,7 +81,7 @@
     position = lax.axis_index("row") * lax.axis_size("head") + lax.axis_index("head")
     share_width = hidden.shape[1] // (lax.axis_size("row") * lax.axis_size("head"))
     vocab_here = w_vocab.shape[0]
-    projection = lax.psum(partial_terms, ("row", "head"))
+    projection = lax.psum(lax.psum(partial_terms, "head"), "row")
     new_full = (stream + projection).astype(jnp.bfloat16)
     final_feat = rms_round(new_full.astype(jnp.float32), final_gain)
     logits = jnp.einsum("sd,vd->sv", final_feat, w_vocab, preferred_element_type=jnp.float32)

time: 281 us -> 283 us (level)
  waiting for transfers between devices: 161 us -> 164 us
    psum x1 -> x2, waiting for transfers between devices: 90.6 us -> 92 us  [per_device(): projection = lax.psum(lax.psum(partial_terms, 'head'), 'row')]
  transfers between devices with their start and end apart: 2 -> 3, of which waited for: 2 -> 3; matrix products, arithmetic and copies ran while one was open for 0% -> 0% of each run, Pallas kernels for 0% -> 0%
where the time goes in v1:
time: 283 us; the launch traced here: 282 us
  waiting for transfers between devices  164 us (58%)
  blocking collectives  63 us (22%)
  matrix products  23.4 us (8%)
  between operations  14.7 us (5%)
  other arithmetic  9.78 us (3%)
  local copies, waits for them, and re-layouts  7.02 us (2%)
    psum x2, waiting for transfers between devices, per_device(): projection = lax.psum(lax.psum(partial_terms, 'head'), 'row')  92 us
    psum x1, waiting for transfers between devices, per_device(): readout = lax.psum(partial_readout, 'row')  71.9 us
    all_gather x1, blocking collectives, per_device(): lax.all_gather(value_part, 'row', axis=2, tiled=True).astype(jnp.float32)  33 us
    unnamed x1, blocking collectives  30 us
    dot_general x1, matrix products, per_device(): jnp.einsum('sd,vd->sv', final_feat, w_vocab, preferred_element_type=jnp.f...  8.26 us
    dot_general x3, matrix products, project(): jnp.einsum('sd,hjd->shj', normed_in, weights, preferred_element_type=jnp....  7.03 us
  transfers between devices with their start and end apart: 3, of which 3 were waited for; matrix products, arithmetic and copies ran while one was open for 0% of the time, Pallas kernels for 0%

profile of v1, /device:TPU:0, one launch (start us, length us, event | category | flops | bytes accessed | tf_op | source)
XLA Modules:
  0.0 282.1 jit_solution(4863562200008397974)
XLA Ops:
  7.2 0.0 copy-start
  7.2 0.0 all-reduce.8.cloned.1.call-start
  7.2 1.2 fusion.17
  8.5 2.7 convolution_convert_fusion
  11.1 0.1 copy.34
  11.3 33.0 %all_gather.21 = bf16[24,4,512]{0,1,2:T(4,128)(2,1)S(1)} all-gather(bf16[24,4,64]{0,1,2:T(4,128)(2,1)S(1)} %copy.34), channel_id=1, replica_groups=mesh['groups'=2,'row'=8,'head'=2] {'row'}, dimensions={2}, use_global_device_ids=true | all-gather | bytes 110592 | tf_op jit(solution)/shard_map/all_gather | solution.py:65
  44.3 0.3 copy.35
  44.6 0.1 copy.36
  44.7 1.2 fusion.13
  45.9 0.7 subtract_exponential_fusion.1
  46.6 0.1 copy.32
  46.7 2.2 fusion.28
  48.9 2.2 fusion.7
  51.1 3.4 %multiply_add_fusion = f32[24,4,32,512]{3,2,1,0:T(8,128)S(1)} fusion(f32[24,4,32,512]{3,2,1,0:T(8,128)} %param.30, f32[24,4,512]{2,1,0:T(4,128)S(1)} %copy.36, f32[24,4,32]{2,1,0:T(4,128)S(1)} %copy.33, f32[24,4]{1,0:T(8,128)S(1)} %copy.32), kind=kLoop, calls=%fused_computation.10 | loop fusion | flops 4718592 | bytes 12792192 | tf_op jit(solution)/shard_map/add | solution.py:63
  54.5 0.0 copy-start.1
  54.5 2.7 copy-done.1
  57.2 0.0 copy-start.4
  57.2 3.1 %fusion.26 = f32[24,4,1,512]{3,2,1,0:T(1,128)S(1)} fusion(f32[24,4,32,512]{3,2,1,0:T(8,128)S(1)} %multiply_add_fusion, f32[24,4,32,1]{2,0,1,3:T(8,128)S(1)} %fusion.7), kind=kOutput, calls=%fused_computation.46 | convolution fusion | flops 18874368 | bytes 6500352 | tf_op jit(solution)/shard_map/shj,shje->she/dot_general | solution.py:68
  60.4 0.7 copy.47
  61.1 0.0 all-reduce.8.cloned.1.call-update
  61.1 0.0 all-reduce.10.cloned.1.call-start
  61.2 71.9 %all-reduce.8.cloned.1.call-done = f32[24,4,512]{2,0,1:T(8,128)} async-done(((f32[24,4,512]{2,0,1:T(8,128)}), f32[24,4,512]{2,0,1:T(8,128)}) %all-reduce.8.cloned.1.call-update) | async-done | bytes 196624 | tf_op jit(solution)/shard_map/psum | solution.py:71
  133.1 1.0 reduce_sum.55
  134.1 1.1 multiply_reduce_fusion
  135.3 3.8 %convolution_bitcast_fusion = f32[24,4096]{1,0:T(8,128)} fusion(bf16[4,64,4096]{2,1,0:T(8,128)(2,1)S(1)} %copy-done, bf16[4,64,4096]{2,1,0:T(8,128)(2,1)} %param.23, f32[24,4,512]{2,0,1:T(8,128)S(1)} %get-tuple-element.86, s32[]{:T(128)S(6)} %select_n.16, f32[4,64]{1,0:T(4,128)S(1)} %copy-done.6, f32[24,4]{0,1:T(4,128)S(1)} %add_rsqrt_fusion, ...), kind=kOutput, calls=%fused_computation.11 | convolution fusion | flops 101099520 | bytes 4854276 | tf_op jit(solution)/shard_map/shj,hjd->sd/dot_general | solution.py:80
  139.0 0.0 all-reduce.10.cloned.1.call-update
  139.0 0.0 all-reduce.12.cloned.1.call-start
  139.1 17.6 %all-reduce.10.cloned.1.call-done = f32[24,4096]{1,0:T(8,128)} async-done(((f32[24,4096]{1,0:T(8,128)}), f32[24,4096]{1,0:T(8,128)}) %all-reduce.10.cloned.1.call-update) | async-done | bytes 393232 | tf_op jit(solution)/shard_map/psum | solution.py:84
  156.6 0.0 all-reduce.12.cloned.1.call-update
  156.7 0.6 copy.38
  157.3 0.6 dynamic-slice
  158.6 74.4 %all-reduce.12.cloned.1.call-done = f32[24,4096]{1,0:T(8,128)} async-done(((f32[24,4096]{1,0:T(8,128)}), f32[24,4096]{1,0:T(8,128)}) %all-reduce.12.cloned.1.call-update) | async-done | bytes 393232 | tf_op jit(solution)/shard_map/psum | solution.py:84
  233.0 1.2 fusion.14
  234.2 8.3 %fusion.50 = (f32[24]{0:T(128)S(1)}, f32[24,1572]{1,0:T(8,128)S(1)}) fusion(bf16[1572,4096]{1,0:T(8,128)(2,1)} %param.29, bf16[24,4096]{1,0:T(8,128)(2,1)S(1)} %get-tuple-element.84, f32[4096]{0:T(1024)S(1)} %copy-done.4, f32[24]{0:T(128)S(1)} %add_rsqrt_fusion.1), kind=kOutput, calls=%fused_computation.74 | convolution fusion | flops 309498688 | bytes 13241920 | tf_op jit(solution)/shard_map/sd,vd->sv/dot_general | solution.py:87
  242.4 0.2 dynamic-update-slice
  242.7 0.2 select_reduce_fusion
  242.9 0.2 dynamic-update-slice.1
  243.1 0.2 dynamic-update-slice.2
  243.4 30.0 %all-reduce.3 = (f32[384]{0:T(512)S(1)}, f32[384]{0:T(512)S(1)}, f32[384]{0:T(512)S(1)}) all-reduce(f32[384]{0:T(512)S(1)} %dynamic-update-slice, f32[384]{0:T(512)S(1)} %dynamic-update-slice.1, f32[384]{0:T(512)S(1)} %dynamic-update-slice.2), channel_id=2, replica_groups=mesh['groups'=2,'row'=8,'head'=2] {'row','head'}, use_global_device_ids=true, to_apply=%add | all-reduce | flops 1152 | bytes 9216
  273.3 0.1 slice.36
  273.4 0.1 slice.37
  273.5 0.1 slice.38
  273.5 0.6 constant_dynamic-slice_fusion.3
  274.1 0.1 reshape.55
  274.2 0.1 reshape.56
  274.3 0.1 reshape.57
  274.4 0.6 while.14
  275.1 0.5 add_subtract_fusion
  (42 shorter events, 0.5 us)
Async XLA Ops:
  7.2 128.1 %copy-start = (bf16[4,64,4096]{2,1,0:T(8,128)(2,1)S(1)}, bf16[4,64,4096]{2,1,0:T(8,128)(2,1)}, u32[]{:S(2)}) copy-start(bf16[4,64,4096]{2,1,0:T(8,128)(2,1)} %param.24) | copy-start | bytes 6291460
  7.2 125.9 %all-reduce.8.cloned.1.call-start = ((), (), s32[]{:S(2)}) async-start(), calls=%async_computation | async-start | bytes 393216 | tf_op jit(solution)/shard_map/psum | solution.py:71
  46.6 7.9 %copy-start.5 = (f32[24,4]{0,1:T(4,128)}, f32[24,4]{0,1:T(4,128)S(1)}, u32[]{:S(2)}) copy-start(f32[24,4]{0,1:T(4,128)S(1)} %get-tuple-element.88) | copy-start | bytes 1156
  54.5 2.7 copy-start.1
  57.2 78.0 %copy-start.2 = (bf16[24,4096]{1,0:T(8,128)(2,1)S(1)}, bf16[24,4096]{1,0:T(8,128)(2,1)}, u32[]{:S(2)}) copy-start(bf16[24,4096]{1,0:T(8,128)(2,1)} %param.18) | copy-start | bytes 589828
  57.2 78.0 %copy-start.3 = (f32[4096]{0:T(1024)S(1)}, f32[4096]{0:T(1024)}, u32[]{:S(2)}) copy-start(f32[4096]{0:T(1024)} %param.19) | copy-start | bytes 49156
  57.2 78.1 %copy-start.6 = (f32[4,64]{1,0:T(4,128)S(1)}, f32[4,64]{1,0:T(4,128)}, u32[]{:S(2)}) copy-start(f32[4,64]{1,0:T(4,128)} %param.27) | copy-start | bytes 3076
  57.2 100.1 %copy-start.8 = (u32[32]{0:T(128)S(1)}, u32[32]{0:T(128)}, u32[]{:S(2)}) copy-start(u32[32]{0:T(128)} %constant.57) | copy-start | bytes 388
  57.2 101.4 %copy-start.7 = (s32[24]{0:T(128)S(1)}, s32[24]{0:T(128)}, u32[]{:S(2)}) copy-start(s32[24]{0:T(128)} %param.33) | copy-start | bytes 292
  57.2 176.9 %copy-start.4 = (f32[4096]{0:T(1024)S(1)}, f32[4096]{0:T(1024)}, u32[]{:S(2)}) copy-start(f32[4096]{0:T(1024)} %param.28) | copy-start | bytes 49156
  61.1 95.5 %all-reduce.10.cloned.1.call-start = ((), (), s32[]{:S(2)}) async-start(), calls=%async_computation.1 | async-start | bytes 786432 | tf_op jit(solution)/shard_map/psum | solution.py:84
  139.0 93.9 %all-reduce.12.cloned.1.call-start = ((), (), s32[]{:S(2)}) async-start(), calls=%async_computation.2 | async-start | bytes 786432 | tf_op jit(solution)/shard_map/psum | solution.py:84
Sparse Core Ops, SparseCore 0:
  61.2 71.7 all-reduce.7
  139.2 17.4 all-reduce.9
  160.0 72.9 all-reduce.11
